TPU v7x, 32 devices: a whole 2x2x4 slice. The times are simulated.
32 devices in a mesh: chain: 8 (over z, core), bond: 4 (over y, x).
Axes of the slice: x: 2, y: 2, z: 4, core: 2. Of those that a mesh axis runs over, the one named last changes fastest.
Arguments:
- site_tensors: float32 [32, 256, 2, 256], P('chain', 'bond'), may hold values from -20 to 20
- bond_gates: float32 [32, 4, 4], P('chain'), may hold values from -1.5 to 2.5
Outputs:
- state: float32 [32, 256, 2, 256], P('chain', 'bond')
- profile: float32 [32], P('chain')
All inputs are finite; a program needn't handle non-finite values.
Results may differ from a plain program's by a relative error of at most 0.0002.
Values sent between devices are 32-bit elements; how exact they have to be, the bound alone decides.
A program may use at most 64 MiB of HBM per device.

v0:
```python
import functools
import math

import jax
import jax.numpy as jnp
from jax import lax
from jax.experimental import pallas as pl
from jax.experimental.pallas import tpu as pltpu
from jax.sharding import PartitionSpec as P

NS_ITERS = 3
RING = 4
CHUNKS = 4
LANES = 128
EPSILON = 1e-06


def split(value):
    high = value.astype(jnp.bfloat16)
    low = (value - high.astype(jnp.float32)).astype(jnp.bfloat16)
    return (high, low)


def times(a, b):
    (ah, al), (bh, bl) = (a, b)
    return jnp.dot(
        jnp.concatenate([ah, ah, al], axis=1),
        jnp.concatenate([bh, bl, bh], axis=0),
        preferred_element_type=jnp.float32,
    )


def times_transposed(a, b):
    (ah, al), (bh, bl) = (a, b)
    return lax.dot_general(
        jnp.concatenate([ah, ah, al], axis=1),
        jnp.concatenate([bh, bl, bh], axis=1),
        (((1,), (1,)), ((), ())),
        preferred_element_type=jnp.float32,
    )


def update(left, right, gate, on_left):
    width = right.shape[0]
    right_split = split(right)
    theta = times(split(left), right_split) * (1.0 / math.sqrt(width))
    theta = [[theta[u * width:(u + 1) * width, v * width:(v + 1) * width] for v in range(2)] for u in range(2)]
    rows = []
    for s in range(2):
        row = []
        for t in range(2):
            total = None
            for u in range(2):
                for v in range(2):
                    factor = gate[2 * s + t:2 * s + t + 1, 2 * u + v:2 * u + v + 1]
                    term = factor * theta[u][v]
                    total = term if total is None else total + term
            row.append(total)
        rows.append(jnp.concatenate(row, axis=1))
    matrix = split(jnp.concatenate(rows, axis=0))
    projected = times_transposed(matrix, right_split)
    squares = jnp.sum(projected * projected, keepdims=True)
    iterate = projected * (1.0 / jnp.sqrt(squares + EPSILON))
    turned = split(iterate.T)
    iterate = split(iterate)
    gram = times_transposed(turned, turned)
    eye = jnp.where(
        lax.broadcasted_iota(jnp.int32, gram.shape, 0) == lax.broadcasted_iota(jnp.int32, gram.shape, 1),
        jnp.float32(1.5),
        jnp.float32(0.0),
    )
    carried = times(turned, matrix)
    factor = None
    for repeat in range(NS_ITERS):
        step = eye - 0.5 * gram
        factor = step if factor is None else times(split(factor), split(step))
        if repeat < NS_ITERS - 1:
            gram_split = split(gram)
            once = 1.5 * gram - 0.5 * times(gram_split, gram_split)
            gram = 1.5 * once - 0.5 * times(split(once), gram_split)
    factor = split(factor)
    on_left(math.sqrt(2 * width) * times(iterate, factor))
    carried = times(factor, split(carried))
    mean = jnp.sum(carried * carried, keepdims=True) * (1.0 / carried.size)
    scale_norm = jnp.sqrt(mean + EPSILON)
    return (carried * (1.0 / scale_norm), jnp.log(scale_norm))


def order(place):
    return place + (place // 2) * (1 - 2 * (place % 2))


def kernel(
    chains, bonds, rows, width,
    x_ref, gates_ref, out_ref, profile_ref,
    inbuf, gates, xbuf, recv, obuf, wall,
    g_send, g_recv, f_send, f_recv, gate_send, gate_recv,
    m_send, m_recv, h_send, h_recv, o_send, o_recv, w_send, w_recv,
):
    chain, bond = (lax.axis_index("chain"), lax.axis_index("bond"))
    slabs = chains // 2
    slab, core = (chain // 2, chain % 2)
    replica, ring = (bond // RING, order(bond % RING))
    tall = rows * 4
    height = width // CHUNKS
    sibling = {"chain": 2 * slab + 1 - core, "bond": bond}

    def remote(src, dst, send, recv_sem, chain_to, bond_to):
        return pltpu.make_async_remote_copy(
            src_ref=src, dst_ref=dst, send_sem=send, recv_sem=recv_sem,
            device_id={"chain": chain_to, "bond": bond_to},
            device_id_type=pl.DeviceIdType.MESH,
        )

    def landed(ref, sem):
        pltpu.make_async_copy(ref, ref, sem).wait()

    gathers = []
    for j in range(2):
        for r in range(bonds // RING):
            bond_to = r * RING + order(2 * core + j)
            for i in range(2):
                src = x_ref.at[pl.ds((2 * j + i) * tall, tall)]
                dst = inbuf.at[i, pl.ds(bond * tall, tall)]
                copy = remote(src, dst, g_send.at[j, r, i], g_recv.at[bond], 2 * slab + i, bond_to)
                here = pltpu.make_async_copy(src, dst, g_recv.at[bond])
                mine = jnp.logical_and(core == i, bond_to == bond)
                gathers.append((copy, here, mine))
                pl.when(mine)(here.start)
                pl.when(jnp.logical_not(mine))(copy.start)
    gate_here = pltpu.make_async_copy(gates_ref, gates.at[core], gate_recv.at[core])
    gate_here.start()
    gate_copy = remote(gates_ref, gates.at[core], gate_send, gate_recv.at[core], sibling["chain"], bond)
    gate_copy.start()

    forwards = []
    for d in range(bonds):
        origin = lax.rem(bond + d, bonds)
        piece = inbuf.at[core, pl.ds(origin * tall, tall)]
        landed(piece, g_recv.at[origin])
        copy = remote(piece, piece, f_send.at[origin], f_recv.at[origin], sibling["chain"], bond)
        copy.start()
        forwards.append(copy)
    for d in range(bonds):
        origin = lax.rem(bond + d, bonds)
        landed(inbuf.at[1 - core, pl.ds(origin * tall, tall)], f_recv.at[origin])
    landed(gates.at[0], gate_recv.at[0])
    landed(gates.at[1], gate_recv.at[1])

    def spin(i, s):
        return jnp.concatenate(
            [inbuf[i, pl.ds(2 * t + s, width, stride=4), :] for t in range(2)], axis=1
        )

    passed = []

    def send_left(value):
        xbuf[0] = value[:width]
        xbuf[1] = value[width:]
        before = lax.rem(ring + RING - 1, RING)
        slab_to = lax.rem(slab + slabs - jnp.where(ring == 0, 1, 0), slabs)
        bond_to = replica * RING + order(before)
        for q in range(CHUNKS):
            part = pl.ds(q * height, height)
            copy = remote(
                xbuf.at[core, part], recv.at[core, part], m_send.at[q], m_recv.at[q],
                2 * slab_to + core, bond_to,
            )
            copy.start()
            passed.append(copy)

    block = ring // 2
    left = jnp.concatenate([spin(0, 0), spin(0, 1)], axis=0)
    right = jnp.concatenate([spin(1, 0), spin(1, 1)], axis=1)
    new_right, weight_even = update(left, right, gates[block, 2 * (ring % 2)], send_left)

    for q in range(CHUNKS):
        part = recv.at[core, pl.ds(q * height, height)]
        landed(part, m_recv.at[q])
        copy = remote(part, part, h_send.at[q], h_recv.at[q], sibling["chain"], bond)
        copy.start()
        forwards.append(copy)
    for q in range(CHUNKS):
        landed(recv.at[1 - core, pl.ds(q * height, height)], h_recv.at[q])

    outs = []

    def put(h, value_of):
        for s in range(2):
            for t in range(2):
                obuf[h, pl.ds(2 * t + s, width, stride=4), :] = value_of(s, t)
        site = lax.rem(slab * 2 * RING + 2 * ring + 1 + h, 4 * chains)
        chain_to, slot = (site // 4, site % 4)
        for j in range(2):
            bond_to = replica * RING + 2 * j + core
            src = obuf.at[h, pl.ds(bond_to * tall, tall)]
            dst = out_ref.at[pl.ds(slot * tall, tall)]
            copy = remote(src, dst, o_send.at[h, j], o_recv.at[slot], chain_to, bond_to)
            here = pltpu.make_async_copy(src, dst, o_recv.at[slot])
            mine = jnp.logical_and(chain_to == chain, bond_to == bond)
            outs.append((copy, mine))
            pl.when(mine)(here.start)
            pl.when(jnp.logical_not(mine))(copy.start)

    def put_left(value):
        put(0, lambda s, t: value[s * width:(s + 1) * width, t * LANES:(t + 1) * LANES])

    left = jnp.concatenate([new_right[:, :width], new_right[:, width:]], axis=0)
    right = jnp.concatenate([recv[0], recv[1]], axis=1)
    new_right, weight_odd = update(left, right, gates[block, 2 * (ring % 2) + 1], put_left)
    put(1, lambda s, t: new_right[:, s * width + t * LANES:s * width + (t + 1) * LANES])

    row = lax.broadcasted_iota(jnp.int32, (8, LANES), 0)
    lane = lax.broadcasted_iota(jnp.int32, (8, LANES), 1)
    own = wall.at[slab * RING + ring]
    own[...] = jnp.where(row == 0, weight_even, weight_odd)
    weights = []
    for dz in range(slabs):
        for dk in range(RING):
            if dz == 0 and dk == 0:
                continue
            chain_to = 2 * lax.rem(slab + dz, slabs) + core
            bond_to = replica * RING + order(lax.rem(ring + dk, RING))
            at = dz * RING + dk
            copy = remote(own, own, w_send.at[at], w_recv.at[at], chain_to, bond_to)
            copy.start()
            weights.append((copy, dz, dk))
    for copy, dz, dk in weights:
        source = lax.rem(slab + slabs - dz, slabs) * RING + lax.rem(ring + RING - dk, RING)
        landed(wall.at[source], w_recv.at[dz * RING + dk])
    total = jnp.zeros((8, LANES), jnp.float32)
    for e in range(slabs * RING):
        counted = jnp.logical_and(row < 2, 2 * e + row <= 4 * chain + lane)
        total = total + jnp.where(counted, wall[e], 0.0)
    running = jnp.sum(total, axis=0, keepdims=True) * (1.0 / (4 * chains))
    profile_ref[...] = jnp.broadcast_to(running, (8, LANES))

    for slot in range(4):
        landed(out_ref.at[pl.ds(slot * tall, tall)], o_recv.at[slot])
    for copy, here, mine in gathers:
        pl.when(jnp.logical_not(mine))(copy.wait_send)
    gate_copy.wait_send()
    for copy in forwards + passed + [c for c, dz, dk in weights]:
        copy.wait_send()
    for copy, mine in outs:
        pl.when(jnp.logical_not(mine))(copy.wait_send)


def per_device(chains, bonds, site_tensors, bond_gates):
    sites, rows, spins, width = site_tensors.shape
    assert sites == 4 and spins == 2 and width == 2 * LANES and bonds % RING == 0 and chains % 2 == 0
    cut = (sites, rows, spins, width // LANES, LANES)
    flat = site_tensors.reshape(cut).transpose(0, 1, 3, 2, 4).reshape(sites * rows * 4, LANES)
    slabs = chains // 2
    dma = pltpu.SemaphoreType.DMA
    out, profile = pl.pallas_call(
        functools.partial(kernel, chains, bonds, rows, width),
        out_shape=(
            jax.ShapeDtypeStruct(flat.shape, jnp.float32),
            jax.ShapeDtypeStruct((8, LANES), jnp.float32),
        ),
        in_specs=[pl.BlockSpec(memory_space=pl.ANY)] * 2,
        out_specs=(pl.BlockSpec(memory_space=pl.ANY), pl.BlockSpec(memory_space=pltpu.VMEM)),
        scratch_shapes=[
            pltpu.VMEM((2, 4 * width, LANES), jnp.float32),
            pltpu.VMEM((2,) + bond_gates.shape, jnp.float32),
            pltpu.VMEM((2, width, width), jnp.float32),
            pltpu.VMEM((2, width, width), jnp.float32),
            pltpu.VMEM((2, 4 * width, LANES), jnp.float32),
            pltpu.VMEM((slabs * RING, 8, LANES), jnp.float32),
            dma((2, bonds // RING, 2)), dma((bonds,)),
            dma((bonds,)), dma((bonds,)),
            dma, dma((2,)),
            dma((CHUNKS,)), dma((CHUNKS,)),
            dma((CHUNKS,)), dma((CHUNKS,)),
            dma((2, 2)), dma((4,)),
            dma((slabs * RING,)), dma((slabs * RING,)),
        ],
        compiler_params=pltpu.CompilerParams(
            has_side_effects=True, vmem_limit_bytes=48 * 1024 * 1024
        ),
    )(flat, bond_gates)
    cut = (sites, rows, width // LANES, spins, LANES)
    state = out.reshape(cut).transpose(0, 1, 3, 2, 4).reshape(site_tensors.shape)
    return (state, profile[0, :sites])


def solution(mesh):
    chains, bonds = (mesh.shape["chain"], mesh.shape["bond"])
    return jax.shard_map(
        functools.partial(per_device, chains, bonds),
        mesh=mesh,
        in_specs=(P("chain", "bond", None, None), P("chain", None, None)),
        out_specs=(P("chain", "bond", None, None), P("chain")),
        check_vma=False,
    )
```

profile of v0, /device:TPU:0, one launch (start us, length us, event | category | flops | bytes accessed | tf_op | source)
XLA Modules:
  0.0 49.9 jit_solution(11196291011494098915)
XLA Ops:
  0.6 0.0 copy-start
  0.6 1.0 %copy-done = f32[4,64,2,256]{3,2,1,0:T(2,128)S(1)} copy-done((f32[4,64,2,256]{3,2,1,0:T(2,128)S(1)}, f32[4,64,2,256]{3,2,1,0:T(2,128)}, u32[]{:S(2)}) %copy-start) | copy-done | bytes 524312
  1.7 0.0 copy-start.1
  1.7 0.7 %copy-done.1 = f32[4,4,4]{2,1,0:T(4,128)S(1)} copy-done((f32[4,4,4]{2,1,0:T(4,128)S(1)}, f32[4,4,4]{2,1,0:T(4,128)}, u32[]{:S(2)}) %copy-start.1) | copy-done | bytes 280
  2.4 46.2 %shard_map.41 = (f32[1024,128]{1,0:T(8,128)S(1)}, f32[8,128]{1,0:T(8,128)S(1)}) custom-call(f32[1024,128]{1,0:T(8,128)S(1)} %bitcast.12, f32[4,4,4]{2,1,0:T(4,128)S(1)} %copy-done.1), custom_call_target="tpu_custom_call" | custom-call | tf_op jit(solution)/shard_map/pallas_call | solution.py:256
  48.5 0.5 %slice_bitcast_fusion = f32[4]{0:T(128)} fusion(f32[8,128]{1,0:T(8,128)S(1)} %get-tuple-element.5), kind=kLoop, calls=%fused_computation | loop fusion | bytes 32 | tf_op jit(solution)/shard_map/squeeze | solution.py:285
  49.1 0.8 %copy.7 = f32[4,64,2,256]{3,2,1,0:T(2,128)} copy(f32[4,64,2,256]{3,2,1,0:T(2,128)S(1)} %bitcast.13) | data formatting | bytes 1048576
Async XLA Ops:
  0.6 1.0 %copy-start = (f32[4,64,2,256]{3,2,1,0:T(2,128)S(1)}, f32[4,64,2,256]{3,2,1,0:T(2,128)}, u32[]{:S(2)}) copy-start(f32[4,64,2,256]{3,2,1,0:T(2,128)} %param.2) | copy-start | bytes 1572868
  1.7 0.7 %copy-start.1 = (f32[4,4,4]{2,1,0:T(4,128)S(1)}, f32[4,4,4]{2,1,0:T(4,128)}, u32[]{:S(2)}) copy-start(f32[4,4,4]{2,1,0:T(4,128)} %gates_ref.1) | copy-start | bytes 772
where the time goes:
time: 50.1 us; the launch traced here: 49.9 us
  Pallas kernels  46.2 us (92%)
  local copies, waits for them, and re-layouts  3.04 us (6%)
  between operations  0.65 us (1%)
    pallas_call x1, Pallas kernels, per_device(): pl.pallas_call(functools.partial(kernel, chains, bonds, rows, width), out...  46.2 us
    unnamed x5, local copies, waits for them, and re-layouts  2.52 us

commit v1 on v0

--- a/solution.py
+++ b/solution.py
@@ -40,25 +40,33 @@
     )
 
 
-def update(left, right, gate, on_left):
+def update(right, lefts, gate, on_left):
     width = right.shape[0]
     right_split = split(right)
-    theta = times(split(left), right_split) * (1.0 / math.sqrt(width))
-    theta = [[theta[u * width:(u + 1) * width, v * width:(v + 1) * width] for v in range(2)] for u in range(2)]
-    rows = []
-    for s in range(2):
-        row = []
-        for t in range(2):
-            total = None
-            for u in range(2):
-                for v in range(2):
-                    factor = gate[2 * s + t:2 * s + t + 1, 2 * u + v:2 * u + v + 1]
-                    term = factor * theta[u][v]
-                    total = term if total is None else total + term
-            row.append(total)
-        rows.append(jnp.concatenate(row, axis=1))
-    matrix = split(jnp.concatenate(rows, axis=0))
-    projected = times_transposed(matrix, right_split)
+    groups = []
+    projected = []
+    for left in lefts:
+        left = left()
+        r = left.shape[0] // 2
+        theta = times(split(left), right_split) * (1.0 / math.sqrt(width))
+        theta = [[theta[u * r:(u + 1) * r, v * width:(v + 1) * width] for v in range(2)] for u in range(2)]
+        rows = []
+        for s in range(2):
+            row = []
+            for t in range(2):
+                total = None
+                for u in range(2):
+                    for v in range(2):
+                        factor = gate[2 * s + t:2 * s + t + 1, 2 * u + v:2 * u + v + 1]
+                        term = factor * theta[u][v]
+                        total = term if total is None else total + term
+                row.append(total)
+            rows.append(jnp.concatenate(row, axis=1))
+        group = split(jnp.concatenate(rows, axis=0))
+        groups.append(group)
+        projected.append(times_transposed(group, right_split))
+    matrix = tuple(jnp.concatenate(part, axis=0) for part in zip(*groups))
+    projected = jnp.concatenate(projected, axis=0)
     squares = jnp.sum(projected * projected, keepdims=True)
     iterate = projected * (1.0 / jnp.sqrt(squares + EPSILON))
     turned = split(iterate.T)
@@ -93,7 +101,7 @@
 def kernel(
     chains, bonds, rows, width,
     x_ref, gates_ref, out_ref, profile_ref,
-    inbuf, gates, xbuf, recv, obuf, wall,
+    slab_sem, ring_sem, fetch_sem, xin, inbuf, gates, xbuf, recv, obuf, wall,
     g_send, g_recv, f_send, f_recv, gate_send, gate_recv,
     m_send, m_recv, h_send, h_recv, o_send, o_recv, w_send, w_recv,
 ):
@@ -115,48 +123,95 @@
     def landed(ref, sem):
         pltpu.make_async_copy(ref, ref, sem).wait()
 
-    gathers = []
-    for j in range(2):
-        for r in range(bonds // RING):
-            bond_to = r * RING + order(2 * core + j)
-            for i in range(2):
-                src = x_ref.at[pl.ds((2 * j + i) * tall, tall)]
-                dst = inbuf.at[i, pl.ds(bond * tall, tall)]
-                copy = remote(src, dst, g_send.at[j, r, i], g_recv.at[bond], 2 * slab + i, bond_to)
-                here = pltpu.make_async_copy(src, dst, g_recv.at[bond])
-                mine = jnp.logical_and(core == i, bond_to == bond)
-                gathers.append((copy, here, mine))
-                pl.when(mine)(here.start)
-                pl.when(jnp.logical_not(mine))(copy.start)
+    fetch = pltpu.make_async_copy(x_ref, xin, fetch_sem)
+    fetch.start()
     gate_here = pltpu.make_async_copy(gates_ref, gates.at[core], gate_recv.at[core])
     gate_here.start()
+    barrier = pltpu.get_barrier_semaphore()
+
+    def greet(semaphore, chain_to, bond_to):
+        to = {"chain": chain_to, "bond": bond_to}
+        pl.semaphore_signal(semaphore, inc=1, device_id=to, device_id_type=pl.DeviceIdType.MESH)
+
+    for db in range(1, bonds):
+        greet(barrier, 2 * slab + 1, lax.rem(bond + db, bonds))
+
+    @pl.when(core == 0)
+    def _():
+        greet(barrier, 2 * slab + 1, bond)
+
+    for dz in range(1, slabs):
+        for db in range(RING):
+            greet(barrier, 2 * lax.rem(slab + dz, slabs), replica * RING + lax.rem(bond + db, RING))
+
+    @pl.when(core == 1)
+    def _():
+        pl.semaphore_wait(barrier, 2 * bonds - 1)
+        greet(slab_sem, 2 * slab, bond)
+
+    @pl.when(core == 0)
+    def _():
+        pl.semaphore_wait(slab_sem, 1)
+
     gate_copy = remote(gates_ref, gates.at[core], gate_send, gate_recv.at[core], sibling["chain"], bond)
     gate_copy.start()
+    fetch.wait()
+
+    short = tall // 2
+    gathers = []
+    for i in (1, 0):
+        for h in range(2):
+            for j in range(2):
+                for r in range(bonds // RING):
+                    bond_to = r * RING + order(2 * core + j)
+                    src = xin.at[pl.ds((2 * j + i) * tall + h * short, short)]
+                    dst = inbuf.at[i, pl.ds(bond * tall + h * short, short)]
+                    sem = g_recv.at[i, bond]
+                    copy = remote(src, dst, g_send.at[i, h, j, r], sem, 2 * slab + h, bond_to)
+                    here = pltpu.make_async_copy(src, dst, sem)
+                    mine = jnp.logical_and(core == h, bond_to == bond)
+                    gathers.append((copy, mine))
+                    pl.when(mine)(here.start)
+                    pl.when(jnp.logical_not(mine))(copy.start)
 
     forwards = []
-    for d in range(bonds):
-        origin = lax.rem(bond + d, bonds)
-        piece = inbuf.at[core, pl.ds(origin * tall, tall)]
-        landed(piece, g_recv.at[origin])
-        copy = remote(piece, piece, f_send.at[origin], f_recv.at[origin], sibling["chain"], bond)
-        copy.start()
-        forwards.append(copy)
-    for d in range(bonds):
-        origin = lax.rem(bond + d, bonds)
-        landed(inbuf.at[1 - core, pl.ds(origin * tall, tall)], f_recv.at[origin])
-    landed(gates.at[0], gate_recv.at[0])
-    landed(gates.at[1], gate_recv.at[1])
-
-    def spin(i, s):
+    part = bonds // 2
+    first = bond // part
+
+    def receive(i, origins):
+        for origin in origins:
+            piece = inbuf.at[i, pl.ds(origin * tall + core * short, short)]
+            landed(piece, g_recv.at[i, origin])
+            copy = remote(
+                piece, piece, f_send.at[i, origin], f_recv.at[i, origin], sibling["chain"], bond
+            )
+            copy.start()
+            forwards.append(copy)
+        for origin in origins:
+            landed(inbuf.at[i, pl.ds(origin * tall + (1 - core) * short, short)], f_recv.at[i, origin])
+
+    def spin(i, s, row, count):
         return jnp.concatenate(
-            [inbuf[i, pl.ds(2 * t + s, width, stride=4), :] for t in range(2)], axis=1
+            [inbuf[i, pl.ds(4 * row + 2 * t + s, count, stride=4), :] for t in range(2)], axis=1
         )
 
+    def meet_ring():
+        @pl.when(core == 0)
+        def _():
+            pl.semaphore_wait(barrier, (slabs - 1) * 2 * RING)
+            greet(ring_sem, 2 * slab + 1, bond)
+
+        @pl.when(core == 1)
+        def _():
+            pl.semaphore_wait(ring_sem, 1)
+
     passed = []
 
     def send_left(value):
-        xbuf[0] = value[:width]
-        xbuf[1] = value[width:]
+        for g in range(2):
+            for s in range(2):
+                here = pl.ds((first + g * (1 - 2 * first)) * half, half)
+                xbuf[s, here] = value[(2 * g + s) * half:(2 * g + s + 1) * half]
         before = lax.rem(ring + RING - 1, RING)
         slab_to = lax.rem(slab + slabs - jnp.where(ring == 0, 1, 0), slabs)
         bond_to = replica * RING + order(before)
@@ -170,9 +225,20 @@
             passed.append(copy)
 
     block = ring // 2
-    left = jnp.concatenate([spin(0, 0), spin(0, 1)], axis=0)
-    right = jnp.concatenate([spin(1, 0), spin(1, 1)], axis=1)
-    new_right, weight_even = update(left, right, gates[block, 2 * (ring % 2)], send_left)
+    half = width // 2
+
+    def left_rows(g):
+        which = first + g * (1 - 2 * first)
+        receive(0, [which * part + lax.rem(bond + d, part) for d in range(part)])
+        return jnp.concatenate([spin(0, s, which * half, half) for s in range(2)], axis=0)
+
+    meet_ring()
+    receive(1, [lax.rem(bond + d, bonds) for d in range(bonds)])
+    landed(gates.at[0], gate_recv.at[0])
+    landed(gates.at[1], gate_recv.at[1])
+    right = jnp.concatenate([spin(1, s, 0, width) for s in range(2)], axis=1)
+    lefts = [functools.partial(left_rows, g) for g in range(2)]
+    new_right, weight_even = update(right, lefts, gates[block, 2 * (ring % 2)], send_left)
 
     for q in range(CHUNKS):
         part = recv.at[core, pl.ds(q * height, height)]
@@ -207,8 +273,7 @@
 
     left = jnp.concatenate([new_right[:, :width], new_right[:, width:]], axis=0)
     right = jnp.concatenate([recv[0], recv[1]], axis=1)
-    new_right, weight_odd = update(left, right, gates[block, 2 * (ring % 2) + 1], put_left)
-    put(1, lambda s, t: new_right[:, s * width + t * LANES:s * width + (t + 1) * LANES])
+    new_right, weight_odd = update(right, [lambda: left], gates[block, 2 * (ring % 2) + 1], put_left)
 
     row = lax.broadcasted_iota(jnp.int32, (8, LANES), 0)
     lane = lax.broadcasted_iota(jnp.int32, (8, LANES), 1)
@@ -225,6 +290,7 @@
             copy = remote(own, own, w_send.at[at], w_recv.at[at], chain_to, bond_to)
             copy.start()
             weights.append((copy, dz, dk))
+    put(1, lambda s, t: new_right[:, s * width + t * LANES:s * width + (t + 1) * LANES])
     for copy, dz, dk in weights:
         source = lax.rem(slab + slabs - dz, slabs) * RING + lax.rem(ring + RING - dk, RING)
         landed(wall.at[source], w_recv.at[dz * RING + dk])
@@ -237,7 +303,7 @@
 
     for slot in range(4):
         landed(out_ref.at[pl.ds(slot * tall, tall)], o_recv.at[slot])
-    for copy, here, mine in gathers:
+    for copy, mine in gathers:
         pl.when(jnp.logical_not(mine))(copy.wait_send)
     gate_copy.wait_send()
     for copy in forwards + passed + [c for c, dz, dk in weights]:
@@ -259,17 +325,21 @@
             jax.ShapeDtypeStruct(flat.shape, jnp.float32),
             jax.ShapeDtypeStruct((8, LANES), jnp.float32),
         ),
-        in_specs=[pl.BlockSpec(memory_space=pl.ANY)] * 2,
+        in_specs=[pl.BlockSpec(memory_space=pltpu.HBM)] * 2,
         out_specs=(pl.BlockSpec(memory_space=pl.ANY), pl.BlockSpec(memory_space=pltpu.VMEM)),
         scratch_shapes=[
+            pltpu.SemaphoreType.REGULAR,
+            pltpu.SemaphoreType.REGULAR,
+            dma,
+            pltpu.VMEM(flat.shape, jnp.float32),
             pltpu.VMEM((2, 4 * width, LANES), jnp.float32),
             pltpu.VMEM((2,) + bond_gates.shape, jnp.float32),
             pltpu.VMEM((2, width, width), jnp.float32),
             pltpu.VMEM((2, width, width), jnp.float32),
             pltpu.VMEM((2, 4 * width, LANES), jnp.float32),
             pltpu.VMEM((slabs * RING, 8, LANES), jnp.float32),
-            dma((2, bonds // RING, 2)), dma((bonds,)),
-            dma((bonds,)), dma((bonds,)),
+            dma((2, 2, 2, bonds // RING)), dma((2, bonds)),
+            dma((2, bonds)), dma((2, bonds)),
             dma, dma((2,)),
             dma((CHUNKS,)), dma((CHUNKS,)),
             dma((CHUNKS,)), dma((CHUNKS,)),
@@ -277,7 +347,7 @@
             dma((slabs * RING,)), dma((slabs * RING,)),
         ],
         compiler_params=pltpu.CompilerParams(
-            has_side_effects=True, vmem_limit_bytes=48 * 1024 * 1024
+            has_side_effects=True, collective_id=0, vmem_limit_bytes=67043328
         ),
     )(flat, bond_gates)
     cut = (sites, rows, width // LANES, spins, LANES)

time: 50.1 us -> 46.4 us (0.926)
  the two profiles are of different devices: /device:TPU:0 before, /device:TPU:11 now
where the time goes in v1:
time: 46.4 us; the launch traced here: 46.2 us
  Pallas kernels  42.4 us (91%)
  local copies, waits for them, and re-layouts  3.2 us (7%)
  between operations  0.64 us (1%)
    pallas_call x1, Pallas kernels, per_device(): pl.pallas_call(functools.partial(kernel, chains, bonds, rows, width), out...  42.4 us
    unnamed x1, local copies, waits for them, and re-layouts  2.01 us
    squeeze x1, local copies, waits for them, and re-layouts, per_device(): return (state, profile[0, :sites])  1.19 us

profile of v1, /device:TPU:11, one launch (start us, length us, event | category | flops | bytes accessed | tf_op | source)
XLA Modules:
  0.0 46.2 jit_solution(9388592138147643572)
XLA Ops:
  0.6 42.4 %shard_map.41 = (f32[1024,128]{1,0:T(8,128)}, f32[8,128]{1,0:T(8,128)}) custom-call(f32[1024,128]{1,0:T(8,128)} %bitcast.12, f32[4,4,4]{2,1,0:T(4,128)} %gates_ref.1), custom_call_target="tpu_custom_call" | custom-call | tf_op jit(solution)/shard_map/pallas_call | solution.py:322
  43.0 1.2 %slice_bitcast_fusion = f32[4]{0:T(128)} fusion(f32[8,128]{1,0:T(8,128)} %get-tuple-element.5), kind=kLoop, calls=%fused_computation | loop fusion | bytes 32 | tf_op jit(solution)/shard_map/squeeze | solution.py:355
  44.2 2.0 %copy.7 = f32[4,64,2,256]{3,2,1,0:T(2,128)} copy(f32[4,64,2,256]{3,2,1,0:T(2,128)} %bitcast.13) | data formatting | bytes 1048576

commit v2 on v1

--- a/solution.py
+++ b/solution.py
@@ -347,7 +347,7 @@
             dma((slabs * RING,)), dma((slabs * RING,)),
         ],
         compiler_params=pltpu.CompilerParams(
-            has_side_effects=True, collective_id=0, vmem_limit_bytes=67043328
+            has_side_effects=True, collective_id=0, vmem_limit_bytes=56_000_000
         ),
     )(flat, bond_gates)
     cut = (sites, rows, width // LANES, spins, LANES)

time: 46.4 us -> 45.2 us (0.974)
  local copies, waits for them, and re-layouts: 3.2 us -> 2 us
    squeeze x1, local copies, waits for them, and re-layouts: 1.19 us -> 0.51 us  [per_device(): return (state, profile[0, :sites])]
    unnamed x1 -> x3, local copies, waits for them, and re-layouts: 2.01 us -> 1.48 us
where the time goes in v2:
time: 45.2 us; the launch traced here: 45 us
  Pallas kernels  42.4 us (94%)
  local copies, waits for them, and re-layouts  2 us (4%)
  between operations  0.65 us (1%)
    pallas_call x1, Pallas kernels, per_device(): pl.pallas_call(functools.partial(kernel, chains, bonds, rows, width), out...  42.4 us
    unnamed x3, local copies, waits for them, and re-layouts  1.48 us

profile of v2, /device:TPU:11, one launch (start us, length us, event | category | flops | bytes accessed | tf_op | source)
XLA Modules:
  0.0 45.0 jit_solution(12360601763123102159)
XLA Ops:
  0.6 0.0 copy-start
  0.6 0.7 %copy-done = f32[4,4,4]{2,1,0:T(4,128)S(1)} copy-done((f32[4,4,4]{2,1,0:T(4,128)S(1)}, f32[4,4,4]{2,1,0:T(4,128)}, u32[]{:S(2)}) %copy-start) | copy-done | bytes 280
  1.3 42.4 %shard_map.41 = (f32[1024,128]{1,0:T(8,128)S(1)}, f32[8,128]{1,0:T(8,128)S(1)}) custom-call(f32[1024,128]{1,0:T(8,128)} %bitcast.13, f32[4,4,4]{2,1,0:T(4,128)S(1)} %copy-done), custom_call_target="tpu_custom_call" | custom-call | tf_op jit(solution)/shard_map/pallas_call | solution.py:322
  43.7 0.5 %slice_bitcast_fusion = f32[4]{0:T(128)} fusion(f32[8,128]{1,0:T(8,128)S(1)} %get-tuple-element.5), kind=kLoop, calls=%fused_computation | loop fusion | bytes 32 | tf_op jit(solution)/shard_map/squeeze | solution.py:355
  44.2 0.8 %copy.7 = f32[4,64,2,256]{3,2,1,0:T(2,128)} copy(f32[4,64,2,256]{3,2,1,0:T(2,128)S(1)} %bitcast.12) | data formatting | bytes 1048576
Async XLA Ops:
  0.6 0.7 %copy-start = (f32[4,4,4]{2,1,0:T(4,128)S(1)}, f32[4,4,4]{2,1,0:T(4,128)}, u32[]{:S(2)}) copy-start(f32[4,4,4]{2,1,0:T(4,128)} %gates_ref.1) | copy-start | bytes 772
